TPU v7x, 32 devices: a whole 2x2x4 slice. The times are simulated.
32 devices in a mesh: seq: 4 (over y, x), seg: 4 (over z), head: 2 (over core).
Axes of the slice: x: 2, y: 2, z: 4, core: 2. Of those that a mesh axis runs over, the one named last changes fastest.
Arguments:
- queries: bfloat16 [8, 16384, 128], P('head', ('seg', 'seq')), may hold values from -6 to 6
- keys: bfloat16 [8, 16384, 128], P('head', ('seg', 'seq')), may hold values from -6 to 6
- values: bfloat16 [8, 16384, 128], P('head', ('seg', 'seq')), may hold values from -8 to 8
- teacher: bfloat16 [8, 16384, 128], P('head', ('seg', 'seq')), may hold values from -6 to 6
- query_proj: float32 [128, 16], replicated, may hold values from -0.5 to 0.5
- key_proj: float32 [128, 16], replicated, may hold values from -0.5 to 0.5
Outputs:
- student: bfloat16 [8, 16384, 128], P('head', ('seg', 'seq'))
- query_grad: float32 [128, 16], replicated
- key_grad: float32 [128, 16], replicated
All inputs are finite; a program needn't handle non-finite values.
Results may differ from a plain program's by a relative error of at most 0.0014.
The roundings to bfloat16 on the way count: a program that leaves them out, or rounds other values in their place, can miss the bound.
Values sent between devices are 32-bit elements; how exact they have to be, the bound alone decides.
No kernel may reach another device: no remote copies, remote signals or barrier semaphores. Data moves between devices by JAX's collectives and lax.ppermute only.
A program may use at most 64 MiB of HBM per device.

v0:
```python
import math
import jax
import jax.numpy as jnp
import numpy as np
from jax import lax
from jax.sharding import PartitionSpec as P

highest = lax.Precision.HIGHEST


def carried_in(value, axis, join, neutral, backward):
    count, mine = (lax.axis_size(axis), lax.axis_index(axis))
    pieces = jax.tree.map(lambda part: lax.all_gather(part, axis), value)
    if backward:
        pieces = jax.tree.map(lambda part: part[::-1], pieces)
        mine = count - 1 - mine
    running = jax.tree.map(
        lambda part, zero: jnp.full_like(part, 0) + jnp.asarray(zero, part.dtype), value, neutral
    )

    def step(position, running):
        longer = join(running, jax.tree.map(lambda part: part[position], pieces))
        return jax.tree.map(lambda new, old: jnp.where(position < mine, new, old), longer, running)

    return lax.fori_loop(0, count - 1, step, running)


def feature_tables(width):
    first, second = np.triu_indices(width)
    eye = np.eye(width)
    coef = np.where(first == second, 0.5**0.5, 1.0)
    return (
        jnp.asarray(eye[first], jnp.float32),
        jnp.asarray(eye[second], jnp.float32),
        jnp.asarray(coef, jnp.float32),
    )


def features(proj_t, tables):
    sel_a, sel_b, coef = tables
    left = jnp.dot(sel_a, proj_t, precision=highest)
    right = jnp.dot(sel_b, proj_t, precision=highest)
    return jnp.concatenate([jnp.ones_like(proj_t[:1]), proj_t, coef[:, None] * left * right], 0)


def feature_grad(proj_t, grad_phi, tables):
    sel_a, sel_b, coef = tables
    width = proj_t.shape[0]
    left = jnp.dot(sel_a, proj_t, precision=highest)
    right = jnp.dot(sel_b, proj_t, precision=highest)
    quad = grad_phi[1 + width :] * coef[:, None]
    return (
        grad_phi[1 : 1 + width]
        + jnp.dot(sel_a.T, quad * right, precision=highest)
        + jnp.dot(sel_b.T, quad * left, precision=highest)
    )


def project(weight_b, rows):
    return lax.dot_general(
        weight_b, rows, (((0,), (1,)), ((), ())), preferred_element_type=jnp.float32
    )


def head_state(q_h, k_h, v_h, wq_b, wk_b, tables):
    q_t = project(wq_b, q_h)
    k_t = project(wk_b, k_h)
    phi_k = features(k_t, tables)
    state = jnp.dot(phi_k.astype(jnp.bfloat16), v_h, preferred_element_type=jnp.float32)
    return (q_t, k_t, state, jnp.sum(phi_k, 1))


def head_forward(q_t, k_t, v_h, teacher_h, s_prev, z_prev, scale, tables):
    phi_q = features(q_t, tables)
    length = q_t.shape[1]
    scores = lax.dot_general(q_t, k_t, (((0,), (0,)), ((), ())), precision=highest)
    causal = jnp.arange(length)[:, None] >= jnp.arange(length)[None, :]
    weights = jnp.where(causal, 1.0 + scores + 0.5 * scores * scores, 0.0)
    numer = jnp.dot(weights.astype(jnp.bfloat16), v_h, preferred_element_type=jnp.float32)
    numer = numer + lax.dot_general(phi_q, s_prev, (((0,), (0,)), ((), ())), precision=highest)
    denom = jnp.sum(weights, 1) + jnp.dot(z_prev, phi_q, precision=highest)
    student = numer / denom[:, None]
    g_out = scale * (student - teacher_h.astype(jnp.float32))
    g_numer = g_out / denom[:, None]
    g_denom = -jnp.sum(g_out * student, 1) / denom
    g_weights = (
        lax.dot_general(
            g_numer.astype(jnp.bfloat16),
            v_h,
            (((1,), (1,)), ((), ())),
            preferred_element_type=jnp.float32,
        )
        + g_denom[:, None]
    )
    g_scores = jnp.where(causal, g_weights * (1.0 + scores), 0.0)
    g_q = lax.dot_general(k_t, g_scores, (((1,), (1,)), ((), ())), precision=highest)
    g_k = jnp.dot(q_t, g_scores, precision=highest)
    g_phi_q = (
        lax.dot_general(s_prev, g_numer, (((1,), (1,)), ((), ())), precision=highest)
        + z_prev[:, None] * g_denom[None, :]
    )
    g_q = g_q + feature_grad(q_t, g_phi_q, tables)
    g_state = jnp.dot(phi_q, g_numer, precision=highest)
    h_state = jnp.dot(phi_q, g_denom, precision=highest)
    return (student, g_q, g_k, g_state, h_state)


def head_grads(q_h, k_h, v_h, k_t, g_q, g_k, g_next, h_next, tables):
    g_phi_k = (
        lax.dot_general(
            g_next.astype(jnp.bfloat16),
            v_h,
            (((1,), (1,)), ((), ())),
            preferred_element_type=jnp.float32,
        )
        + h_next[:, None]
    )
    g_k = g_k + feature_grad(k_t, g_phi_k, tables)
    grad_q = lax.dot_general(
        q_h, g_q.astype(jnp.bfloat16), (((0,), (1,)), ((), ())), preferred_element_type=jnp.float32
    )
    grad_k = lax.dot_general(
        k_h, g_k.astype(jnp.bfloat16), (((0,), (1,)), ((), ())), preferred_element_type=jnp.float32
    )
    return (grad_q, grad_k)


def add_trees(first, second):
    return jax.tree.map(jnp.add, first, second)


def masked_fold(mine, backward, carry, piece):
    rows = piece[0].shape[0]
    index = jnp.arange(rows)
    keep = index > mine if backward else index < mine

    def pick(array):
        shaped = keep.reshape((rows,) + (1,) * (array.ndim - 1))
        return jnp.sum(jnp.where(shaped, array, 0.0), 0)

    part = jax.tree.map(pick, piece)
    whole = jax.tree.map(lambda array: jnp.sum(array, 0), piece)
    return (add_trees(carry[0], part), add_trees(carry[1], whole))


def carried(local, backward):
    zeros = jax.tree.map(jnp.zeros_like, local)
    stacked = jax.tree.map(lambda array: array[None], local)
    inner, totals = masked_fold(
        lax.axis_index("seq"),
        backward,
        (zeros, zeros),
        (
            lax.all_gather(stacked[0], "seq", axis=0, tiled=True),
            lax.all_gather(stacked[1], "seq", axis=0, tiled=True),
        ),
    )
    outer = carried_in(totals, "seg", add_trees, zeros, backward)
    return add_trees(inner, outer)


def shards(queries, keys, values, teacher, query_proj, key_proj):
    tables = feature_tables(query_proj.shape[1])
    wq_b = query_proj.astype(jnp.bfloat16)
    wk_b = key_proj.astype(jnp.bfloat16)
    q_t, k_t, states, counts = lax.map(
        lambda xs: head_state(xs[0], xs[1], xs[2], wq_b, wk_b, tables), (queries, keys, values)
    )
    s_prev, z_prev = carried((states, counts), False)
    heads_all = queries.shape[0] * lax.axis_size("head")
    tokens_all = queries.shape[1] * lax.axis_size("seq") * lax.axis_size("seg")
    scale = 1.0 / math.sqrt(heads_all * tokens_all)
    student, g_q, g_k, g_state, h_state = lax.map(
        lambda xs: head_forward(xs[0], xs[1], xs[2], xs[3], xs[4], xs[5], scale, tables),
        (q_t, k_t, values, teacher, s_prev, z_prev),
    )
    g_next, h_next = carried((g_state, h_state), True)
    grad_q, grad_k = lax.map(
        lambda xs: head_grads(xs[0], xs[1], xs[2], xs[3], xs[4], xs[5], xs[6], xs[7], tables),
        (queries, keys, values, k_t, g_q, g_k, g_next, h_next),
    )
    summed = lax.psum((jnp.sum(grad_q, 0), jnp.sum(grad_k, 0)), ("seq", "seg", "head"))
    return (student.astype(jnp.bfloat16), summed[0], summed[1])


def solution(mesh):
    in_specs = (
        P("head", ("seg", "seq"), None),
        P("head", ("seg", "seq"), None),
        P("head", ("seg", "seq"), None),
        P("head", ("seg", "seq"), None),
        P(),
        P(),
    )
    out_specs = (P("head", ("seg", "seq"), None), P(), P())
    return jax.shard_map(shards, mesh=mesh, in_specs=in_specs, out_specs=out_specs, check_vma=False)
```

profile of v0, /device:TPU:0, one launch (start us, length us, event | category | flops | bytes accessed | tf_op | source)
XLA Modules:
  0.0 344.7 jit_solution(8274270570329167139)
XLA Ops:
  8.7 27.1 %while.81 = (s32[]{:T(128)}, f32[4,16,1024]{2,1,0:T(8,128)S(1)}, f32[4,16,1024]{2,1,0:T(8,128)S(1)}, f32[4,153,128]{2,1,0:T(8,128)S(1)}, f32[4,153]{1,0:T(4,128)...) while((s32[]{:T(128)}, f32[4,16,1024]{2,1,0:T(8,128)S(1)}, ...), condition=%wide.region_2.3_spmd.clone, body=%wide.region_0.2_spmd.sunk.clone.sunk | while | flops 103662440 | bytes 4145861 | solution.py:166
  11.0 1.5 convolution_multiply_fusion.7
  12.5 1.5 fusion.187
  13.9 1.3 fusion.188
  17.7 1.5 convolution_multiply_fusion.7
  19.2 1.5 fusion.187
  20.7 1.3 fusion.188
  24.5 1.5 convolution_multiply_fusion.7
  26.0 1.5 fusion.187
  27.5 1.3 fusion.188
  31.3 1.5 convolution_multiply_fusion.7
  32.8 1.5 fusion.187
  34.3 1.3 fusion.188
  36.6 31.5 %all-gather.17.cloned.1.call-done = f32[16,153,128]{2,1,0:T(8,128)} async-done(((f32[4,153,128]{2,1,0:T(8,128)}), f32[16,153,128]{2,1,0:T(8,128)}) %all-gather.17.cloned.1.call-update) | async-done | bytes 1253392 | tf_op jit(solution)/shard_map/all_gather | solution.py:154
  68.1 2.4 fusion.90
  70.6 8.1 %all-gather.8 = f32[4,4,153]{2,1,0:T(4,128)S(1)} all-gather(f32[1,4,153]{2,1,0:T(4,128)S(1)} %bitcast.304), channel_id=4, replica_groups=mesh['seq'=4,'seg'=4,'head'=2] {'seq'}, dimensions={0}, use_global_device_ids=true | all-gather | bytes 12240 | tf_op jit(solution)/shard_map/all_gather | solution.py:155
  78.8 13.7 %all-gather.9 = f32[4,4,153]{2,1,0:T(4,128)S(1)} all-gather(f32[1,4,153]{2,1,0:T(4,128)S(1)} %bitcast.301), channel_id=5, replica_groups=mesh['seq'=4,'seg'=4,'head'=2] {'seg'}, dimensions={0}, use_global_device_ids=true | all-gather | bytes 12240 | tf_op jit(solution)/shard_map/all_gather | solution.py:13
  93.2 10.2 %all-gather.19.cloned.1.call-done = f32[16,153,128]{2,1,0:T(8,128)} async-done(((f32[4,153,128]{2,1,0:T(8,128)}), f32[16,153,128]{2,1,0:T(8,128)}) %all-gather.19.cloned.1.call-update) | async-done | bytes 1253392 | tf_op jit(solution)/shard_map/all_gather | solution.py:13
  103.4 3.4 while.84
  109.1 98.5 %while.82 = (s32[]{:T(128)}, bf16[4,1024,128]{2,1,0:T(8,128)(2,1)}, bf16[4,16,1024]{2,1,0:T(8,128)(2,1)}, f32[4,16,1024]{2,1,0:T(8,128)}, f32[4,153,128]{2,1,0:T...) while((s32[]{:T(128)}, bf16[4,1024,128]{2,1,0:T(8,128)(2,1)}, ...), condition=%wide.region_12.13_spmd.clone, body=%wide.region_9.12_spmd.sunk.clone.sunk | while | flops 1998507008 | bytes 75882544 | solution.py:173
  110.4 3.8 %fusion.212 = (f32[1024]{0:T(1024)S(1)}, f32[1024,1024]{0,1:T(8,128)S(1)}) fusion(f32[16,1024]{1,0:T(8,128)S(1)} %dynamic-slice_bitcast_fusion.2, f32[4,16,1024]{2,1,0:T(8,128)S(1)} %get-tuple-element.1167, s32[]{:T(128)S(6)} %copy.77), kind=kOutput, calls=%fused_computation.28.clone.1 | convolution fusion | flops 208665600 | bytes 4329476 | tf_op jit(solution)/shard_map/while/body/eval_jaxpr/dot_general | solution.py:76
  116.0 1.6 fusion.215
  117.6 1.8 fusion.216
  120.3 2.1 convolution_add_fusion.13
  123.5 1.8 multiply_select_fusion.2
  125.3 2.1 fusion.217
  127.4 4.2 %fusion.218 = f32[4,16,1024]{2,1,0:T(8,128)} fusion(f32[4,16,1024]{2,1,0:T(8,128)} %get-tuple-element.1144, s32[]{:T(128)S(6)} %copy.77, f32[16,1024]{1,0:T(8,128)S(1)} %dynamic-slice_bitcast_fusion.2, f32[1024,1024]{0,1:T(8,128)S(1)} %multiply_select_fusion.2), kind=kOutput, calls=%fused_computation.37.clone.1 | convolution fusion | flops 201326592 | bytes 4325380 | tf_op jit(solution)/shard_map/while/body/eval_jaxpr/dot_general | solution.py:97
  131.6 1.4 fusion.219
  134.9 3.8 %fusion.212 = (f32[1024]{0:T(1024)S(1)}, f32[1024,1024]{0,1:T(8,128)S(1)}) fusion(f32[16,1024]{1,0:T(8,128)S(1)} %dynamic-slice_bitcast_fusion.2, f32[4,16,1024]{2,1,0:T(8,128)S(1)} %get-tuple-element.1167, s32[]{:T(128)S(6)} %copy.77), kind=kOutput, calls=%fused_computation.28.clone.1 | convolution fusion | flops 208665600 | bytes 4329476 | tf_op jit(solution)/shard_map/while/body/eval_jaxpr/dot_general | solution.py:76
  140.6 1.6 fusion.215
  142.2 1.8 fusion.216
  144.8 2.1 convolution_add_fusion.13
  148.0 1.8 multiply_select_fusion.2
  149.9 2.1 fusion.217
  152.0 4.2 %fusion.218 = f32[4,16,1024]{2,1,0:T(8,128)} fusion(f32[4,16,1024]{2,1,0:T(8,128)} %get-tuple-element.1144, s32[]{:T(128)S(6)} %copy.77, f32[16,1024]{1,0:T(8,128)S(1)} %dynamic-slice_bitcast_fusion.2, f32[1024,1024]{0,1:T(8,128)S(1)} %multiply_select_fusion.2), kind=kOutput, calls=%fused_computation.37.clone.1 | convolution fusion | flops 201326592 | bytes 4325380 | tf_op jit(solution)/shard_map/while/body/eval_jaxpr/dot_general | solution.py:97
  156.1 1.4 fusion.219
  159.5 3.8 %fusion.212 = (f32[1024]{0:T(1024)S(1)}, f32[1024,1024]{0,1:T(8,128)S(1)}) fusion(f32[16,1024]{1,0:T(8,128)S(1)} %dynamic-slice_bitcast_fusion.2, f32[4,16,1024]{2,1,0:T(8,128)S(1)} %get-tuple-element.1167, s32[]{:T(128)S(6)} %copy.77), kind=kOutput, calls=%fused_computation.28.clone.1 | convolution fusion | flops 208665600 | bytes 4329476 | tf_op jit(solution)/shard_map/while/body/eval_jaxpr/dot_general | solution.py:76
  165.1 1.6 fusion.215
  166.7 1.8 fusion.216
  169.4 2.1 convolution_add_fusion.13
  172.5 1.8 multiply_select_fusion.2
  174.4 2.1 fusion.217
  176.5 4.2 %fusion.218 = f32[4,16,1024]{2,1,0:T(8,128)} fusion(f32[4,16,1024]{2,1,0:T(8,128)} %get-tuple-element.1144, s32[]{:T(128)S(6)} %copy.77, f32[16,1024]{1,0:T(8,128)S(1)} %dynamic-slice_bitcast_fusion.2, f32[1024,1024]{0,1:T(8,128)S(1)} %multiply_select_fusion.2), kind=kOutput, calls=%fused_computation.37.clone.1 | convolution fusion | flops 201326592 | bytes 4325380 | tf_op jit(solution)/shard_map/while/body/eval_jaxpr/dot_general | solution.py:97
  180.7 1.4 fusion.219
  184.0 3.8 %fusion.212 = (f32[1024]{0:T(1024)S(1)}, f32[1024,1024]{0,1:T(8,128)S(1)}) fusion(f32[16,1024]{1,0:T(8,128)S(1)} %dynamic-slice_bitcast_fusion.2, f32[4,16,1024]{2,1,0:T(8,128)S(1)} %get-tuple-element.1167, s32[]{:T(128)S(6)} %copy.77), kind=kOutput, calls=%fused_computation.28.clone.1 | convolution fusion | flops 208665600 | bytes 4329476 | tf_op jit(solution)/shard_map/while/body/eval_jaxpr/dot_general | solution.py:76
  189.6 1.6 fusion.215
  191.2 1.8 fusion.216
  193.9 2.1 convolution_add_fusion.13
  197.1 1.8 multiply_select_fusion.2
  198.9 2.1 fusion.217
  201.0 4.2 %fusion.218 = f32[4,16,1024]{2,1,0:T(8,128)} fusion(f32[4,16,1024]{2,1,0:T(8,128)} %get-tuple-element.1144, s32[]{:T(128)S(6)} %copy.77, f32[16,1024]{1,0:T(8,128)S(1)} %dynamic-slice_bitcast_fusion.2, f32[1024,1024]{0,1:T(8,128)S(1)} %multiply_select_fusion.2), kind=kOutput, calls=%fused_computation.37.clone.1 | convolution fusion | flops 201326592 | bytes 4325380 | tf_op jit(solution)/shard_map/while/body/eval_jaxpr/dot_general | solution.py:97
  205.2 1.4 fusion.219
  207.7 27.9 %all-gather.21.cloned.1.call-done = f32[16,153,128]{2,1,0:T(8,128)} async-done(((f32[4,153,128]{2,1,0:T(8,128)}), f32[16,153,128]{2,1,0:T(8,128)}) %all-gather.21.cloned.1.call-update) | async-done | bytes 1253392 | tf_op jit(solution)/shard_map/all_gather | solution.py:154
  235.6 2.3 fusion.89
  238.0 8.1 %all-gather.10 = f32[4,4,153]{2,1,0:T(4,128)S(1)} all-gather(f32[1,4,153]{2,1,0:T(4,128)S(1)} %bitcast.303), channel_id=8, replica_groups=mesh['seq'=4,'seg'=4,'head'=2] {'seq'}, dimensions={0}, use_global_device_ids=true | all-gather | bytes 12240 | tf_op jit(solution)/shard_map/all_gather | solution.py:155
  246.2 13.7 %all-gather.11 = f32[4,4,153]{2,1,0:T(4,128)S(1)} all-gather(f32[1,4,153]{2,1,0:T(4,128)S(1)} %bitcast.302), channel_id=9, replica_groups=mesh['seq'=4,'seg'=4,'head'=2] {'seg'}, dimensions={0}, use_global_device_ids=true | all-gather | bytes 12240 | tf_op jit(solution)/shard_map/all_gather | solution.py:13
  259.9 10.9 %all-gather.23.cloned.1.call-done = f32[16,153,128]{2,1,0:T(8,128)} async-done(((f32[4,153,128]{2,1,0:T(8,128)}), f32[16,153,128]{2,1,0:T(8,128)}) %all-gather.23.cloned.1.call-update) | async-done | bytes 1253392 | tf_op jit(solution)/shard_map/all_gather | solution.py:13
  270.8 1.4 rev.6
  272.7 25.7 %while.83 = (s32[]{:T(128)}, f32[4,128,16]{1,2,0:T(8,128)S(1)}, f32[4,128,16]{1,2,0:T(8,128)S(1)}, bf16[4,1024,128]{2,1,0:T(8,128)(2,1)}, bf16[4,16,1024]{2,1,0:...) while((s32[]{:T(128)}, f32[4,128,16]{1,2,0:T(8,128)S(1)}, ...), condition=%wide.region_20.21_spmd.clone, body=%wide.region_19.20_spmd.sunk.clone.sunk | while | flops 156230656 | bytes 5469037 | solution.py:178
  276.8 1.3 fusion.236
  283.2 1.3 fusion.236
  289.6 1.3 fusion.236
  296.0 1.3 fusion.236
  298.4 39.8 %all-reduce = (f32[128,16]{0,1:T(8,128)}, f32[128,16]{0,1:T(8,128)}) all-reduce(f32[128,16]{0,1:T(8,128)S(1)} %reduce_sum.125, f32[128,16]{0,1:T(8,128)S(1)} %reduce_sum.126), channel_id=1, replica_groups=mesh['seq'=4,'seg'=4,'head'=2] {'seq','seg','head'}, use_global_device_ids=true, to_apply=%region_22.23 | all-reduce | flops 4096 | bytes 32768 | tf_op jit(solution)/shard_map/psum | solution.py:182
  (201 shorter events, 62.6 us)
Async XLA Ops:
  7.2 61.0 %all-gather.17.cloned.1.call-start = ((), (), s32[]{:S(2)}) async-start(), calls=%async_computation | async-start | bytes 1638400 | tf_op jit(solution)/shard_map/all_gather | solution.py:154
  35.8 0.7 copy-start.4
  36.6 66.9 %all-gather.19.cloned.1.call-start = ((), (), s32[]{:S(2)}) async-start(), calls=%async_computation.1 | async-start | bytes 1638400 | tf_op jit(solution)/shard_map/all_gather | solution.py:13
  68.1 40.9 %copy-start.2 = (f32[136,16]{1,0:T(8,128)S(1)}, f32[136,16]{1,0:T(8,128)}, u32[]{:S(2)}) copy-start(f32[136,16]{1,0:T(8,128)} %get-tuple-element.1252) | copy-start | bytes 26116
  68.1 40.9 %copy-start.3 = (f32[136,16]{1,0:T(8,128)S(1)}, f32[136,16]{1,0:T(8,128)}, u32[]{:S(2)}) copy-start(f32[136,16]{1,0:T(8,128)} %get-tuple-element.1254) | copy-start | bytes 26116
  68.1 40.9 %copy-start.5 = (f32[136]{0:T(256)S(1)}, f32[136]{0:T(256)}, u32[]{:S(2)}) copy-start(f32[136]{0:T(256)} %get-tuple-element.1271) | copy-start | bytes 1636
  70.5 165.0 %all-gather.21.cloned.1.call-start = ((), (), s32[]{:S(2)}) async-start(), calls=%async_computation.2 | async-start | bytes 1638400 | tf_op jit(solution)/shard_map/all_gather | solution.py:154
  114.3 3.4 copy-start
  119.6 3.9 %copy-start.1 = (f32[1024,1024]{0,1:T(8,128)S(1)}, f32[1024,1024]{0,1:T(8,128)}, u32[]{:S(2)}) copy-start(f32[1024,1024]{0,1:T(8,128)} %copy-done) | copy-start | bytes 12582916 | tf_op jit(solution)/shard_map/while
  123.5 1.9 copy-start.6
  127.4 6.3 %copy-start.7 = (bf16[4,16,1024]{2,1,0:T(8,128)(2,1)}, bf16[4,16,1024]{2,1,0:T(8,128)(2,1)S(1)}, u32[]{:S(2)}) copy-start(bf16[4,16,1024]{2,1,0:T(8,128)(2,1)S(1)} %fusion.217) | copy-start | bytes 393220 | tf_op jit(solution)/shard_map/while
  138.8 3.4 copy-start
  144.1 3.9 %copy-start.1 = (f32[1024,1024]{0,1:T(8,128)S(1)}, f32[1024,1024]{0,1:T(8,128)}, u32[]{:S(2)}) copy-start(f32[1024,1024]{0,1:T(8,128)} %copy-done) | copy-start | bytes 12582916 | tf_op jit(solution)/shard_map/while
  148.0 1.9 copy-start.6
  152.0 6.3 %copy-start.7 = (bf16[4,16,1024]{2,1,0:T(8,128)(2,1)}, bf16[4,16,1024]{2,1,0:T(8,128)(2,1)S(1)}, u32[]{:S(2)}) copy-start(bf16[4,16,1024]{2,1,0:T(8,128)(2,1)S(1)} %fusion.217) | copy-start | bytes 393220 | tf_op jit(solution)/shard_map/while
  163.3 3.4 copy-start
  168.6 3.9 %copy-start.1 = (f32[1024,1024]{0,1:T(8,128)S(1)}, f32[1024,1024]{0,1:T(8,128)}, u32[]{:S(2)}) copy-start(f32[1024,1024]{0,1:T(8,128)} %copy-done) | copy-start | bytes 12582916 | tf_op jit(solution)/shard_map/while
  172.5 1.9 copy-start.6
  176.5 6.3 %copy-start.7 = (bf16[4,16,1024]{2,1,0:T(8,128)(2,1)}, bf16[4,16,1024]{2,1,0:T(8,128)(2,1)S(1)}, u32[]{:S(2)}) copy-start(bf16[4,16,1024]{2,1,0:T(8,128)(2,1)S(1)} %fusion.217) | copy-start | bytes 393220 | tf_op jit(solution)/shard_map/while
  187.8 3.4 copy-start
  193.2 3.9 %copy-start.1 = (f32[1024,1024]{0,1:T(8,128)S(1)}, f32[1024,1024]{0,1:T(8,128)}, u32[]{:S(2)}) copy-start(f32[1024,1024]{0,1:T(8,128)} %copy-done) | copy-start | bytes 12582916 | tf_op jit(solution)/shard_map/while
  197.1 1.9 copy-start.6
  201.0 6.3 %copy-start.7 = (bf16[4,16,1024]{2,1,0:T(8,128)(2,1)}, bf16[4,16,1024]{2,1,0:T(8,128)(2,1)S(1)}, u32[]{:S(2)}) copy-start(bf16[4,16,1024]{2,1,0:T(8,128)(2,1)S(1)} %fusion.217) | copy-start | bytes 393220 | tf_op jit(solution)/shard_map/while
  207.6 63.2 %all-gather.23.cloned.1.call-start = ((), (), s32[]{:S(2)}) async-start(), calls=%async_computation.3 | async-start | bytes 1638400 | tf_op jit(solution)/shard_map/all_gather | solution.py:13
Sparse Core Ops, SparseCore 0:
  36.7 31.3 all-gather.16
  70.7 32.7 all-gather.18
  207.7 27.7 all-gather.20
  238.1 32.7 all-gather.22
where the time goes:
time: 347 us; the launch traced here: 345 us
  matrix products  140 us (40%)
  blocking collectives  83.4 us (24%)
  waiting for transfers between devices  80.6 us (23%)
  between operations  14 us (4%)
  other arithmetic  12.4 us (4%)
  local copies, waits for them, and re-layouts  12.3 us (4%)
    all_gather x2, waiting for transfers between devices, carried(): lax.all_gather(stacked[0], 'seq', axis=0, tiled=True)  59.4 us
    psum x1, blocking collectives, shards(): lax.psum((jnp.sum(grad_q, 0), jnp.sum(grad_k, 0)), ('seq', 'seg', 'head'))  39.8 us
    all_gather x2, blocking collectives, carried_in(): pieces = jax.tree.map(lambda part: lax.all_gather(part, axis), value)  27.4 us
    all_gather x2, waiting for transfers between devices, carried_in(): pieces = jax.tree.map(lambda part: lax.all_gather(part, axis), value)  21.2 us
    dot_general x4, matrix products, head_forward(): g_k = jnp.dot(q_t, g_scores, precision=highest)  16.6 us
    all_gather x2, blocking collectives, carried(): lax.all_gather(stacked[1], 'seq', axis=0, tiled=True)  16.3 us
    dot_general x4, matrix products, head_forward(): lax.dot_general(q_t, k_t, (((0,), (0,)), ((), ())), precision=highest)  15.3 us
    dot_general x8, matrix products, project(): lax.dot_general(weight_b, rows, (((0,), (1,)), ((), ())), preferred_eleme...  9.01 us
  transfers between devices with their start and end apart: 4, of which 4 were waited for; matrix products, arithmetic and copies ran while one was open for 0% of the time, Pallas kernels for 0%

commit v1 on v0

--- a/solution.py
+++ b/solution.py
@@ -1,3 +1,4 @@
+import functools
 import math
 import jax
 import jax.numpy as jnp
@@ -6,6 +7,24 @@
 from jax.sharding import PartitionSpec as P
 
 highest = lax.Precision.HIGHEST
+
+
+def _read_vector(sheet, peer_axis):
+    after = jax.lax.axis_size(peer_axis)
+    latest = jax.lax.axis_index(peer_axis)
+    carry_out, then = (after, latest)
+    long_array, field_out = (sheet, 1)
+    while field_out < carry_out:
+        all_values = list(map(lambda k0: (k0, k0 ^ field_out), range(carry_out)))
+        next_value = jax.lax.ppermute(long_array, peer_axis, all_values)
+        far_arr = jnp.concatenate([long_array, next_value], axis=0)
+        w1 = jnp.concatenate([next_value, long_array], axis=0)
+        long_array = jnp.where(then & field_out == 0, far_arr, w1)
+        field_out = 2 * field_out
+    return long_array
+
+
+plate_begin = functools.partial(_read_vector, peer_axis="seq")
 
 
 def carried_in(value, axis, join, neutral, backward):
@@ -150,10 +169,7 @@
         lax.axis_index("seq"),
         backward,
         (zeros, zeros),
-        (
-            lax.all_gather(stacked[0], "seq", axis=0, tiled=True),
-            lax.all_gather(stacked[1], "seq", axis=0, tiled=True),
-        ),
+        (plate_begin(stacked[0]), lax.all_gather(stacked[1], "seq", axis=0, tiled=True)),
     )
     outer = carried_in(totals, "seg", add_trees, zeros, backward)
     return add_trees(inner, outer)

time: 347 us -> 362 us (1.043)
  local copies, waits for them, and re-layouts: 12.3 us -> 48.9 us
  waiting for transfers between devices: 80.6 us -> 63.4 us
  matrix products: 140 us -> 129 us
  starting transfers between devices: 0.16 us -> 7.93 us
    all_gather x2 -> x0, waiting for transfers between devices: 59.4 us -> none  [carried(): lax.all_gather(stacked[0], 'seq', axis=0, tiled=True)]
    ppermute x0 -> x4, waiting for transfers between devices: none -> 40.8 us  [_read_vector(): next_value = jax.lax.ppermute(long_array, peer_axis, all_values)]
    dynamic_update_slice x8 -> x24, local copies, waits for them, and re-layouts: 0.35 us -> 31 us  [shards(): lax.map(lambda xs: head_state(xs[0], xs[1], xs[2], wq_b, wk_b, tables), (...]
    ppermute x0 -> x4, starting transfers between devices: none -> 7.85 us  [_read_vector(): next_value = jax.lax.ppermute(long_array, peer_axis, all_values)]
    dot_general x4, matrix products: 8.28 us -> 2.89 us  [head_forward(): lax.dot_general(s_prev, g_numer, (((1,), (1,)), ((), ())), precision=high...]
    dynamic_slice x8 -> x16, local copies, waits for them, and re-layouts: 0.06 us -> 4.59 us  [shards(): lax.map(lambda xs: head_forward(xs[0], xs[1], xs[2], xs[3], xs[4], xs[5],...]
  transfers between devices with their start and end apart: 4 -> 6, of which waited for: 4 -> 6; matrix products, arithmetic and copies ran while one was open for 0% -> 0% of each run, Pallas kernels for 0% -> 0%
where the time goes in v1:
time: 362 us; the launch traced here: 360 us
  matrix products  129 us (36%)
  blocking collectives  84 us (23%)
  waiting for transfers between devices  63.4 us (18%)
  local copies, waits for them, and re-layouts  48.9 us (14%)
  between operations  14.2 us (4%)
  other arithmetic  10.9 us (3%)
  starting transfers between devices  7.93 us (2%)
    ppermute x4, waiting for transfers between devices, _read_vector(): next_value = jax.lax.ppermute(long_array, peer_axis, all_values)  40.8 us
    psum x1, blocking collectives, shards(): lax.psum((jnp.sum(grad_q, 0), jnp.sum(grad_k, 0)), ('seq', 'seg', 'head'))  39.8 us
    dynamic_update_slice x24, local copies, waits for them, and re-layouts, shards(): lax.map(lambda xs: head_state(xs[0], xs[1], xs[2], wq_b, wk_b, tables), (...  31 us
    all_gather x2, blocking collectives, carried_in(): pieces = jax.tree.map(lambda part: lax.all_gather(part, axis), value)  27.7 us
    all_gather x2, waiting for transfers between devices, carried_in(): pieces = jax.tree.map(lambda part: lax.all_gather(part, axis), value)  22.6 us
    dot_general x4, matrix products, head_forward(): g_k = jnp.dot(q_t, g_scores, precision=highest)  16.6 us
    all_gather x2, blocking collectives, carried(): lax.all_gather(stacked[1], 'seq', axis=0, tiled=True)  16.6 us
    dot_general x4, matrix products, head_forward(): lax.dot_general(q_t, k_t, (((0,), (0,)), ((), ())), precision=highest)  15.3 us
  transfers between devices with their start and end apart: 6, of which 6 were waited for; matrix products, arithmetic and copies ran while one was open for 0% of the time, Pallas kernels for 0%

profile of v1, /device:TPU:0, one launch (start us, length us, event | category | flops | bytes accessed | tf_op | source)
XLA Modules:
  0.0 359.7 jit_solution(15789962234656111245)
XLA Ops:
  8.7 38.0 %while.81 = (s32[]{:T(128)}, f32[4,16,1024]{2,1,0:T(8,128)S(1)}, f32[4,16,1024]{2,1,0:T(8,128)S(1)}, f32[4,153,128]{2,0,1:T(4,128)S(1)}, f32[4,153]{1,0:T(4,128)...) while((s32[]{:T(128)}, f32[4,16,1024]{2,1,0:T(8,128)S(1)}, ...), condition=%wide.region_2.3_spmd.clone, body=%wide.region_0.2_spmd.sunk.clone.sunk | while | flops 103662440 | bytes 4454193 | solution.py:182
  11.0 1.5 convolution_multiply_fusion.7
  12.5 1.5 fusion.176
  15.3 2.6 dynamic_update_slice.80
  20.5 1.5 convolution_multiply_fusion.7
  22.0 1.5 fusion.176
  24.8 2.6 dynamic_update_slice.80
  30.0 1.5 convolution_multiply_fusion.7
  31.5 1.5 fusion.176
  34.3 2.6 dynamic_update_slice.80
  39.5 1.5 convolution_multiply_fusion.7
  40.9 1.5 fusion.176
  43.8 2.6 dynamic_update_slice.80
  46.7 3.0 collective-permute-start
  49.7 7.4 %collective-permute-done = f32[1,4,153,128]{3,1,2,0:T(4,128)S(1)} collective-permute-done((f32[1,4,153,128]{3,1,2,0:T(4,128)S(1)}, f32[1,4,153,128]{3,1,2,0:T(4,128)S(1)}, u32[]{:S(2)}, u32[]{:S(2)}) %collective-permute-start) | collective-permute-done | bytes 313376 | tf_op jit(solution)/shard_map/ppermute | solution.py:19
  57.3 1.8 collective-permute-start.1
  59.1 13.5 %collective-permute-done.1 = f32[2,4,153,128]{3,1,2,0:T(4,128)S(1)} collective-permute-done((f32[2,4,153,128]{3,1,2,0:T(4,128)S(1)}, f32[2,4,153,128]{3,1,2,0:T(4,128)S(1)}, u32[]{:S(2)}, u32[]{:S(2)}) %collective-permute-start.1) | collective-permute-done | bytes 626720 | tf_op jit(solution)/shard_map/ppermute | solution.py:19
  74.2 8.2 %all-gather.6 = f32[4,4,153]{2,1,0:T(4,128)S(1)} all-gather(f32[1,4,153]{2,1,0:T(4,128)S(1)} %bitcast.301), channel_id=3, replica_groups=mesh['seq'=4,'seg'=4,'head'=2] {'seq'}, dimensions={0}, use_global_device_ids=true | all-gather | bytes 12240 | tf_op jit(solution)/shard_map/all_gather | solution.py:172
  82.5 13.7 %all-gather.7 = f32[4,4,153]{2,1,0:T(4,128)S(1)} all-gather(f32[1,4,153]{2,1,0:T(4,128)S(1)} %bitcast.298), channel_id=4, replica_groups=mesh['seq'=4,'seg'=4,'head'=2] {'seg'}, dimensions={0}, use_global_device_ids=true | all-gather | bytes 12240 | tf_op jit(solution)/shard_map/all_gather | solution.py:32
  96.9 11.4 %all-gather.13.cloned.1.call-done = f32[16,153,128]{2,1,0:T(8,128)} async-done(((f32[4,153,128]{2,1,0:T(8,128)}), f32[16,153,128]{2,1,0:T(8,128)}) %all-gather.13.cloned.1.call-update) | async-done | bytes 1253392 | tf_op jit(solution)/shard_map/all_gather | solution.py:32
  108.3 3.4 while.84
  114.7 110.8 %while.82 = (s32[]{:T(128)}, bf16[4,1024,128]{2,1,0:T(8,128)(2,1)}, bf16[4,16,1024]{2,1,0:T(8,128)(2,1)}, f32[4,16,1024]{2,1,0:T(8,128)}, f32[4,153,128]{2,0,1:T...) while((s32[]{:T(128)}, bf16[4,1024,128]{2,1,0:T(8,128)(2,1)}, ...), condition=%wide.region_12.13_spmd.clone, body=%wide.region_9.12_spmd.sunk.clone.sunk | while | flops 1998507008 | bytes 76341792 | solution.py:189
  116.1 3.8 %fusion.199 = (f32[1024]{0:T(1024)S(1)}, f32[1024,1024]{0,1:T(8,128)S(1)}) fusion(f32[16,1024]{1,0:T(8,128)S(1)} %dynamic-slice_bitcast_fusion.2, f32[4,16,1024]{2,1,0:T(8,128)S(1)} %get-tuple-element.1190, s32[]{:T(128)S(6)} %copy.117), kind=kOutput, calls=%fused_computation.27.clone.1 | convolution fusion | flops 208665600 | bytes 4329476 | tf_op jit(solution)/shard_map/while/body/eval_jaxpr/dot_general | solution.py:95
  121.7 1.6 fusion.202
  127.9 1.8 multiply_select_fusion.2
  129.8 2.1 fusion.204
  131.9 4.2 %fusion.205 = f32[4,16,1024]{2,1,0:T(8,128)} fusion(f32[4,16,1024]{2,1,0:T(8,128)} %get-tuple-element.1167, s32[]{:T(128)S(6)} %copy.117, f32[16,1024]{1,0:T(8,128)S(1)} %dynamic-slice_bitcast_fusion.2, f32[1024,1024]{0,1:T(8,128)S(1)} %multiply_select_fusion.2), kind=kOutput, calls=%fused_computation.35.clone.1 | convolution fusion | flops 201326592 | bytes 4325380 | tf_op jit(solution)/shard_map/while/body/eval_jaxpr/dot_general | solution.py:116
  136.9 3.6 %dynamic_update_slice.85 = f32[4,153,128]{2,0,1:T(4,128)} dynamic-update-slice(f32[4,153,128]{2,0,1:T(4,128)} %get-tuple-element.1168, f32[1,153,128]{2,0,1:T(1,128)S(1)} %copy.74, s32[]{:T(128)S(6)} %copy.117, s32[]{:T(128)} %constant.132.clone.1..sunk.1, s32[]{:T(128)} %constant.132.clone.1..sunk.1) | dynamic-update-slice | bytes 156676 | tf_op jit(solution)/shard_map/while/body/jit(dynamic_update_index_in_dim)/dynamic_update_slice | solution.py:182
  141.2 1.3 dynamic_update_slice.86
  143.7 3.8 %fusion.199 = (f32[1024]{0:T(1024)S(1)}, f32[1024,1024]{0,1:T(8,128)S(1)}) fusion(f32[16,1024]{1,0:T(8,128)S(1)} %dynamic-slice_bitcast_fusion.2, f32[4,16,1024]{2,1,0:T(8,128)S(1)} %get-tuple-element.1190, s32[]{:T(128)S(6)} %copy.117), kind=kOutput, calls=%fused_computation.27.clone.1 | convolution fusion | flops 208665600 | bytes 4329476 | tf_op jit(solution)/shard_map/while/body/eval_jaxpr/dot_general | solution.py:95
  149.3 1.6 fusion.202
  155.6 1.8 multiply_select_fusion.2
  157.5 2.1 fusion.204
  159.6 4.2 %fusion.205 = f32[4,16,1024]{2,1,0:T(8,128)} fusion(f32[4,16,1024]{2,1,0:T(8,128)} %get-tuple-element.1167, s32[]{:T(128)S(6)} %copy.117, f32[16,1024]{1,0:T(8,128)S(1)} %dynamic-slice_bitcast_fusion.2, f32[1024,1024]{0,1:T(8,128)S(1)} %multiply_select_fusion.2), kind=kOutput, calls=%fused_computation.35.clone.1 | convolution fusion | flops 201326592 | bytes 4325380 | tf_op jit(solution)/shard_map/while/body/eval_jaxpr/dot_general | solution.py:116
  164.6 3.6 %dynamic_update_slice.85 = f32[4,153,128]{2,0,1:T(4,128)} dynamic-update-slice(f32[4,153,128]{2,0,1:T(4,128)} %get-tuple-element.1168, f32[1,153,128]{2,0,1:T(1,128)S(1)} %copy.74, s32[]{:T(128)S(6)} %copy.117, s32[]{:T(128)} %constant.132.clone.1..sunk.1, s32[]{:T(128)} %constant.132.clone.1..sunk.1) | dynamic-update-slice | bytes 156676 | tf_op jit(solution)/shard_map/while/body/jit(dynamic_update_index_in_dim)/dynamic_update_slice | solution.py:182
  168.9 1.3 dynamic_update_slice.86
  171.4 3.8 %fusion.199 = (f32[1024]{0:T(1024)S(1)}, f32[1024,1024]{0,1:T(8,128)S(1)}) fusion(f32[16,1024]{1,0:T(8,128)S(1)} %dynamic-slice_bitcast_fusion.2, f32[4,16,1024]{2,1,0:T(8,128)S(1)} %get-tuple-element.1190, s32[]{:T(128)S(6)} %copy.117), kind=kOutput, calls=%fused_computation.27.clone.1 | convolution fusion | flops 208665600 | bytes 4329476 | tf_op jit(solution)/shard_map/while/body/eval_jaxpr/dot_general | solution.py:95
  177.0 1.6 fusion.202
  183.3 1.8 multiply_select_fusion.2
  185.1 2.1 fusion.204
  187.2 4.2 %fusion.205 = f32[4,16,1024]{2,1,0:T(8,128)} fusion(f32[4,16,1024]{2,1,0:T(8,128)} %get-tuple-element.1167, s32[]{:T(128)S(6)} %copy.117, f32[16,1024]{1,0:T(8,128)S(1)} %dynamic-slice_bitcast_fusion.2, f32[1024,1024]{0,1:T(8,128)S(1)} %multiply_select_fusion.2), kind=kOutput, calls=%fused_computation.35.clone.1 | convolution fusion | flops 201326592 | bytes 4325380 | tf_op jit(solution)/shard_map/while/body/eval_jaxpr/dot_general | solution.py:116
  192.3 3.6 %dynamic_update_slice.85 = f32[4,153,128]{2,0,1:T(4,128)} dynamic-update-slice(f32[4,153,128]{2,0,1:T(4,128)} %get-tuple-element.1168, f32[1,153,128]{2,0,1:T(1,128)S(1)} %copy.74, s32[]{:T(128)S(6)} %copy.117, s32[]{:T(128)} %constant.132.clone.1..sunk.1, s32[]{:T(128)} %constant.132.clone.1..sunk.1) | dynamic-update-slice | bytes 156676 | tf_op jit(solution)/shard_map/while/body/jit(dynamic_update_index_in_dim)/dynamic_update_slice | solution.py:182
  196.6 1.3 dynamic_update_slice.86
  199.0 3.8 %fusion.199 = (f32[1024]{0:T(1024)S(1)}, f32[1024,1024]{0,1:T(8,128)S(1)}) fusion(f32[16,1024]{1,0:T(8,128)S(1)} %dynamic-slice_bitcast_fusion.2, f32[4,16,1024]{2,1,0:T(8,128)S(1)} %get-tuple-element.1190, s32[]{:T(128)S(6)} %copy.117), kind=kOutput, calls=%fused_computation.27.clone.1 | convolution fusion | flops 208665600 | bytes 4329476 | tf_op jit(solution)/shard_map/while/body/eval_jaxpr/dot_general | solution.py:95
  204.7 1.6 fusion.202
  210.9 1.8 multiply_select_fusion.2
  212.8 2.1 fusion.204
  214.9 4.2 %fusion.205 = f32[4,16,1024]{2,1,0:T(8,128)} fusion(f32[4,16,1024]{2,1,0:T(8,128)} %get-tuple-element.1167, s32[]{:T(128)S(6)} %copy.117, f32[16,1024]{1,0:T(8,128)S(1)} %dynamic-slice_bitcast_fusion.2, f32[1024,1024]{0,1:T(8,128)S(1)} %multiply_select_fusion.2), kind=kOutput, calls=%fused_computation.35.clone.1 | convolution fusion | flops 201326592 | bytes 4325380 | tf_op jit(solution)/shard_map/while/body/eval_jaxpr/dot_general | solution.py:116
  219.9 3.6 %dynamic_update_slice.85 = f32[4,153,128]{2,0,1:T(4,128)} dynamic-update-slice(f32[4,153,128]{2,0,1:T(4,128)} %get-tuple-element.1168, f32[1,153,128]{2,0,1:T(1,128)S(1)} %copy.74, s32[]{:T(128)S(6)} %copy.117, s32[]{:T(128)} %constant.132.clone.1..sunk.1, s32[]{:T(128)} %constant.132.clone.1..sunk.1) | dynamic-update-slice | bytes 156676 | tf_op jit(solution)/shard_map/while/body/jit(dynamic_update_index_in_dim)/dynamic_update_slice | solution.py:182
  224.2 1.3 dynamic_update_slice.86
  225.6 1.4 collective-permute-start.2
  227.0 7.1 %collective-permute-done.2 = f32[1,4,153,128]{3,1,2,0:T(4,128)S(1)} collective-permute-done((f32[1,4,153,128]{3,1,2,0:T(4,128)}, f32[1,4,153,128]{3,1,2,0:T(4,128)S(1)}, u32[]{:S(2)}, u32[]{:S(2)}) %collective-permute-start.2) | collective-permute-done | bytes 313376 | tf_op jit(solution)/shard_map/ppermute | solution.py:19
  235.4 1.6 collective-permute-start.3
  237.0 12.7 %collective-permute-done.3 = f32[2,4,153,128]{3,1,2,0:T(4,128)S(1)} collective-permute-done((f32[2,4,153,128]{3,1,2,0:T(4,128)S(1)}, f32[2,4,153,128]{3,1,2,0:T(4,128)S(1)}, u32[]{:S(2)}, u32[]{:S(2)}) %collective-permute-start.3) | collective-permute-done | bytes 626720 | tf_op jit(solution)/shard_map/ppermute | solution.py:19
  251.2 8.4 %all-gather.8 = f32[4,4,153]{2,1,0:T(4,128)S(1)} all-gather(f32[1,4,153]{2,1,0:T(4,128)} %bitcast.300), channel_id=6, replica_groups=mesh['seq'=4,'seg'=4,'head'=2] {'seq'}, dimensions={0}, use_global_device_ids=true | all-gather | bytes 12240 | tf_op jit(solution)/shard_map/all_gather | solution.py:172
  259.7 14.0 %all-gather.9 = f32[4,4,153]{2,1,0:T(4,128)S(1)} all-gather(f32[1,4,153]{2,1,0:T(4,128)S(1)} %bitcast.299), channel_id=7, replica_groups=mesh['seq'=4,'seg'=4,'head'=2] {'seg'}, dimensions={0}, use_global_device_ids=true | all-gather | bytes 12240 | tf_op jit(solution)/shard_map/all_gather | solution.py:32
  273.7 11.2 %all-gather.15.cloned.1.call-done = f32[16,153,128]{2,1,0:T(8,128)} async-done(((f32[4,153,128]{2,1,0:T(8,128)}), f32[16,153,128]{2,1,0:T(8,128)}) %all-gather.15.cloned.1.call-update) | async-done | bytes 1253392 | tf_op jit(solution)/shard_map/all_gather | solution.py:32
  284.9 1.4 rev.6
  287.0 26.0 %while.83 = (s32[]{:T(128)}, f32[4,128,16]{1,2,0:T(8,128)S(1)}, f32[4,128,16]{1,2,0:T(8,128)S(1)}, bf16[4,1024,128]{2,1,0:T(8,128)(2,1)}, bf16[4,16,1024]{2,1,0:...) while((s32[]{:T(128)}, f32[4,128,16]{1,2,0:T(8,128)S(1)}, ...), condition=%wide.region_20.21_spmd.clone, body=%wide.region_19.20_spmd.sunk.clone.sunk | while | flops 156230656 | bytes 5544153 | solution.py:194
  291.1 1.3 fusion.222
  297.6 1.3 fusion.222
  304.1 1.3 fusion.222
  310.6 1.3 fusion.222
  313.1 39.8 %all-reduce = (f32[128,16]{0,1:T(8,128)}, f32[128,16]{0,1:T(8,128)}) all-reduce(f32[128,16]{0,1:T(8,128)S(1)} %reduce_sum.125, f32[128,16]{0,1:T(8,128)S(1)} %reduce_sum.126), channel_id=1, replica_groups=mesh['seq'=4,'seg'=4,'head'=2] {'seq','seg','head'}, use_global_device_ids=true, to_apply=%region_22.23 | all-reduce | flops 4096 | bytes 32768 | tf_op jit(solution)/shard_map/psum | solution.py:198
  (229 shorter events, 86.7 us)
Async XLA Ops:
  7.2 101.1 %all-gather.13.cloned.1.call-start = ((), (), s32[]{:S(2)}) async-start(), calls=%async_computation | async-start | bytes 1638400 | tf_op jit(solution)/shard_map/all_gather | solution.py:32
  46.7 10.4 %collective-permute-start = (f32[1,4,153,128]{3,1,2,0:T(4,128)S(1)}, f32[1,4,153,128]{3,1,2,0:T(4,128)S(1)}, u32[]{:S(2)}, u32[]{:S(2)}) collective-permute-start(f32[1,4,153,128]{3,1,2,0:T(4,128)S(1)} %bitcast.291), channel_id=1, source_target_pairs={{0,8},{8,0},{16,24},{24,16},{1,9},{9,1},{17,25},{25,17},{2,10},{10... | collective-permute-start | bytes 940040 | tf_op jit(solution)/shard_map/ppermute | solution.py:19
  57.3 15.4 %collective-permute-start.1 = (f32[2,4,153,128]{3,1,2,0:T(4,128)S(1)}, f32[2,4,153,128]{3,1,2,0:T(4,128)S(1)}, u32[]{:S(2)}, u32[]{:S(2)}) collective-permute-start(f32[2,4,153,128]{3,1,2,0:T(4,128)S(1)} %maximum_select_fusion.2), channel_id=1, source_target_pairs={{0,16},{8,24},{16,0},{24,8},{1,17},{9,25},{17,1},{25,9},{2,18},{10... | collective-permute-start | bytes 1880072 | tf_op jit(solution)/shard_map/ppermute | solution.py:19
  73.3 41.4 %copy-start.2 = (f32[136,16]{1,0:T(8,128)S(1)}, f32[136,16]{1,0:T(8,128)}, u32[]{:S(2)}) copy-start(f32[136,16]{1,0:T(8,128)} %get-tuple-element.1273) | copy-start | bytes 26116
  73.3 41.4 %copy-start.3 = (f32[136,16]{1,0:T(8,128)S(1)}, f32[136,16]{1,0:T(8,128)}, u32[]{:S(2)}) copy-start(f32[136,16]{1,0:T(8,128)} %get-tuple-element.1275) | copy-start | bytes 26116
  73.4 41.4 %copy-start.4 = (f32[136]{0:T(256)S(1)}, f32[136]{0:T(256)}, u32[]{:S(2)}) copy-start(f32[136]{0:T(256)} %get-tuple-element.1290) | copy-start | bytes 1636
  74.2 210.7 %all-gather.15.cloned.1.call-start = ((), (), s32[]{:S(2)}) async-start(), calls=%async_computation.1 | async-start | bytes 1638400 | tf_op jit(solution)/shard_map/all_gather | solution.py:32
  119.9 3.4 copy-start
  125.4 2.6 copy-start.1
  127.9 1.9 copy-start.5
  131.9 10.7 %copy-start.6 = (bf16[4,16,1024]{2,1,0:T(8,128)(2,1)}, bf16[4,16,1024]{2,1,0:T(8,128)(2,1)S(1)}, u32[]{:S(2)}) copy-start(bf16[4,16,1024]{2,1,0:T(8,128)(2,1)S(1)} %fusion.204) | copy-start | bytes 393220 | tf_op jit(solution)/shard_map/while
  147.6 3.4 copy-start
  153.0 2.6 copy-start.1
  155.6 1.9 copy-start.5
  159.6 10.7 %copy-start.6 = (bf16[4,16,1024]{2,1,0:T(8,128)(2,1)}, bf16[4,16,1024]{2,1,0:T(8,128)(2,1)S(1)}, u32[]{:S(2)}) copy-start(bf16[4,16,1024]{2,1,0:T(8,128)(2,1)S(1)} %fusion.204) | copy-start | bytes 393220 | tf_op jit(solution)/shard_map/while
  175.2 3.4 copy-start
  180.7 2.6 copy-start.1
  183.3 1.9 copy-start.5
  187.2 10.7 %copy-start.6 = (bf16[4,16,1024]{2,1,0:T(8,128)(2,1)}, bf16[4,16,1024]{2,1,0:T(8,128)(2,1)S(1)}, u32[]{:S(2)}) copy-start(bf16[4,16,1024]{2,1,0:T(8,128)(2,1)S(1)} %fusion.204) | copy-start | bytes 393220 | tf_op jit(solution)/shard_map/while
  202.9 3.4 copy-start
  208.4 2.6 copy-start.1
  210.9 1.9 copy-start.5
  214.9 10.7 %copy-start.6 = (bf16[4,16,1024]{2,1,0:T(8,128)(2,1)}, bf16[4,16,1024]{2,1,0:T(8,128)(2,1)S(1)}, u32[]{:S(2)}) copy-start(bf16[4,16,1024]{2,1,0:T(8,128)(2,1)S(1)} %fusion.204) | copy-start | bytes 393220 | tf_op jit(solution)/shard_map/while
  225.6 8.6 %collective-permute-start.2 = (f32[1,4,153,128]{3,1,2,0:T(4,128)}, f32[1,4,153,128]{3,1,2,0:T(4,128)S(1)}, u32[]{:S(2)}, u32[]{:S(2)}) collective-permute-start(f32[1,4,153,128]{3,1,2,0:T(4,128)} %bitcast.289), channel_id=1, source_target_pairs={{0,8},{8,0},{16,24},{24,16},{1,9},{9,1},{17,25},{25,17},{2,10},{10... | collective-permute-start | bytes 940040 | tf_op jit(solution)/shard_map/ppermute | solution.py:19
  235.4 14.3 %collective-permute-start.3 = (f32[2,4,153,128]{3,1,2,0:T(4,128)S(1)}, f32[2,4,153,128]{3,1,2,0:T(4,128)S(1)}, u32[]{:S(2)}, u32[]{:S(2)}) collective-permute-start(f32[2,4,153,128]{3,1,2,0:T(4,128)S(1)} %maximum_select_fusion.3), channel_id=1, source_target_pairs={{0,16},{8,24},{16,0},{24,8},{1,17},{9,25},{17,1},{25,9},{2,18},{10... | collective-permute-start | bytes 1880072 | tf_op jit(solution)/shard_map/ppermute | solution.py:19
Sparse Core Ops, SparseCore 0:
  74.3 33.9 all-gather.12
  251.3 33.5 all-gather.14
